TPU v7x, 32 devices: a whole 2x2x4 slice. The times are simulated.
32 devices in a mesh: cell: 8 (over z, x), grp: 4 (over y, core).
Axes of the slice: x: 2, y: 2, z: 4, core: 2. Of those that a mesh axis runs over, the one named last changes fastest.
Arguments:
- atom_sites: float32 [3, 16384], P(None, ('cell', 'grp')), may hold values from 0 to 8, as said below
- grid_points: float32 [3, 12288], P(None, ('cell', 'grp')), may hold values from 0 to 8, as said below
- dipole_guess: float32 [3, 16384], P(None, ('cell', 'grp')), may hold values from -2 to 2
- fixed_field: float32 [3, 16384], P(None, ('cell', 'grp')), may hold values from -1800 to 1800
- polarisability: float32 [16384], P(('cell', 'grp')), may hold values from 0.0005 to 0.002
- base_charge: float32 [12288], P(('cell', 'grp')), may hold values from -12 to 12
- response: float32 [12288], P(('cell', 'grp')), may hold values from 0.02 to 0.2
- near_blocks: int32 [128, 8], P(('cell', 'grp')), may hold values from 0 to 47, as said below
- grid_blocks: int32 [128, 4], P(('cell', 'grp')), may hold values from 0 to 35, as said below
- source_blocks: int32 [96, 8], P(('cell', 'grp')), may hold values from 0 to 47, as said below
Outputs:
- dipoles: float32 [3, 16384], P(None, ('cell', 'grp'))
- qm_charges: float32 [12288], P(('cell', 'grp'))
Inputs may be any that keep to these rules, and one draw needn't show every extreme that they name: `atom_sites`: atom a has first coordinate in [c, c + 1) with c = a // 2048, the other two in [0, 1). `grid_points`: grid point g has first coordinate in [c, c + 1) with c = g // 1536, the other two in [0, 1). `near_blocks`: each row holds 8 distinct MM window indices, never the block's own index 16 + b % 16. `grid_blocks`: each row holds 4 distinct grid window indices. `source_blocks`: each row holds 8 distinct MM window indices.
All inputs are finite; a program needn't handle non-finite values.
Results may differ from a plain program's by a relative error of at most 0.0003.
Values sent between devices are 32-bit elements; how exact they have to be, the bound alone decides.
A program may use at most 64 MiB of HBM per device.

v0:
```python
import jax
import jax.numpy as jnp
from jax import lax
from jax.sharding import PartitionSpec as P

BLOCK = 128
ITERS = 3
soften_sq = 0.04


def with_halo(x, sides, width):
    for axis, dim in sides:
        peers, length = (lax.axis_size(axis), x.shape[dim])
        up = [(i, (i + 1) % peers) for i in range(peers - 1)]
        down = [(j, i) for i, j in up]
        last = lax.slice_in_dim(x, length - width, length, axis=dim)
        initial = lax.slice_in_dim(x, 0, width, axis=dim)
        before = lax.ppermute(last, axis, up)
        after = lax.ppermute(initial, axis, down)
        x = jnp.concatenate([before, x, after], axis=dim)
    return x


def pair_geometry(targets, sources):
    delta_x = targets[0][:, None] - sources[0][None, :]
    delta_y = targets[1][:, None] - sources[1][None, :]
    delta_z = targets[2][:, None] - sources[2][None, :]
    inverse = 1.0 / jnp.sqrt(delta_x * delta_x + delta_y * delta_y + delta_z * delta_z + soften_sq)
    inv_cube = inverse * inverse * inverse
    return (delta_x, delta_y, delta_z, inv_cube, inv_cube * inverse * inverse)


def dipole_field(targets, sources, moments, keep_mask):
    delta_x, delta_y, delta_z, inv_cube, inv_fifth = pair_geometry(targets, sources)
    projected = (
        moments[0][None, :] * delta_x
        + moments[1][None, :] * delta_y
        + moments[2][None, :] * delta_z
    )
    radial = 3.0 * projected * inv_fifth * keep_mask
    direct = inv_cube * keep_mask
    return jnp.stack(
        [
            jnp.sum(radial * delta_x - moments[0][None, :] * direct, axis=1),
            jnp.sum(radial * delta_y - moments[1][None, :] * direct, axis=1),
            jnp.sum(radial * delta_z - moments[2][None, :] * direct, axis=1),
        ]
    )


def charge_field(targets, sources, charges):
    delta_x, delta_y, delta_z, inv_cube, inv_fifth = pair_geometry(targets, sources)
    weight = charges[None, :] * inv_cube
    return jnp.stack(
        [
            jnp.sum(weight * delta_x, axis=1),
            jnp.sum(weight * delta_y, axis=1),
            jnp.sum(weight * delta_z, axis=1),
        ]
    )


def dipole_potential(targets, sources, moments):
    delta_x, delta_y, delta_z, inv_cube, inv_fifth = pair_geometry(targets, sources)
    projected = (
        moments[0][None, :] * delta_x
        + moments[1][None, :] * delta_y
        + moments[2][None, :] * delta_z
    )
    return jnp.sum(projected * inv_cube, axis=1)


def far_geometry(targets, cell_here, cell_count):
    centres = jnp.arange(cell_count, dtype=jnp.int32).astype(jnp.float32) + 0.5
    delta_x = targets[0][None, :] - centres[:, None]
    delta_y = targets[1][None, :] - 0.5
    delta_z = targets[2][None, :] - 0.5
    far_mask = (jnp.abs(jnp.arange(cell_count, dtype=jnp.int32) - cell_here) >= 2).astype(
        jnp.float32
    )[:, None]
    inverse = 1.0 / jnp.sqrt(delta_x * delta_x + delta_y * delta_y + delta_z * delta_z + soften_sq)
    inv_cube = inverse * inverse * inverse * far_mask
    return (delta_x, delta_y, delta_z, inv_cube, inv_cube * inverse * inverse)


def far_field(targets, cell_here, moments, charges):
    delta_x, delta_y, delta_z, inv_cube, inv_fifth = far_geometry(
        targets, cell_here, charges.shape[0]
    )
    projected = moments[:, 0:1] * delta_x + moments[:, 1:2] * delta_y + moments[:, 2:3] * delta_z
    radial = 3.0 * projected * inv_fifth
    coulomb = charges[:, None] * inv_cube
    return jnp.stack(
        [
            jnp.sum(radial * delta_x - moments[:, 0:1] * inv_cube + coulomb * delta_x, axis=0),
            jnp.sum(radial * delta_y - moments[:, 1:2] * inv_cube + coulomb * delta_y, axis=0),
            jnp.sum(radial * delta_z - moments[:, 2:3] * inv_cube + coulomb * delta_z, axis=0),
        ]
    )


def far_potential(targets, cell_here, moments):
    delta_x, delta_y, delta_z, inv_cube, inv_fifth = far_geometry(
        targets, cell_here, moments.shape[0]
    )
    projected = moments[:, 0:1] * delta_x + moments[:, 1:2] * delta_y + moments[:, 2:3] * delta_z
    return jnp.sum(projected * inv_cube, axis=0)


def listed_tiles(tile_set, index_lists):
    taken = jnp.take(tile_set, index_lists, axis=1)
    count, listed = index_lists.shape
    return jnp.transpose(taken, (1, 0, 2, 3)).reshape(count, 3, listed * tile_set.shape[2])


def spread(payload):
    lifted = payload[:, None, None, :]
    with_rims = with_halo(lifted, (("cell", 1),), 1)
    return lax.all_gather(with_rims, "grp", axis=2, tiled=True)


def body(
    atom_sites,
    grid_points,
    dipole_guess,
    fixed_field,
    polarisability,
    base_charge,
    response,
    near_blocks,
    grid_blocks,
    source_blocks,
):
    groups = lax.axis_size("grp")
    cell_here = lax.axis_index("cell")
    grp_here = lax.axis_index("grp")
    local_blocks = near_blocks.shape[0]
    local_gblocks = source_blocks.shape[0]
    atom_count = atom_sites.shape[1]
    grid_count = grid_points.shape[1]
    cell_blocks = local_blocks * groups
    cell_gblocks = local_gblocks * groups
    statics = spread(jnp.concatenate([atom_sites, grid_points], axis=1))
    site_tiles = statics[:, :, :, :atom_count].reshape(3, 3 * cell_blocks, BLOCK)
    point_tiles = statics[:, :, :, atom_count:].reshape(3, 3 * cell_gblocks, BLOCK)
    atom_targets = jnp.transpose(atom_sites.reshape(3, local_blocks, BLOCK), (1, 0, 2))
    grid_targets = jnp.transpose(grid_points.reshape(3, local_gblocks, BLOCK), (1, 0, 2))
    own_slots = cell_blocks + grp_here * local_blocks + jnp.arange(local_blocks, dtype=jnp.int32)
    atom_lists = jnp.concatenate([own_slots[:, None], near_blocks], axis=1)
    near_sites = listed_tiles(site_tiles, atom_lists)
    grid_sites = listed_tiles(point_tiles, grid_blocks)
    source_sites = listed_tiles(site_tiles, source_blocks)
    keep_mask = jnp.concatenate(
        [
            1.0 - jnp.eye(BLOCK, dtype=jnp.float32),
            jnp.ones((BLOCK, near_blocks.shape[1] * BLOCK), jnp.float32),
        ],
        axis=1,
    )
    centre = jnp.stack(
        [
            cell_here.astype(jnp.float32) + 0.5,
            jnp.array(0.5, jnp.float32),
            jnp.array(0.5, jnp.float32),
        ]
    )
    offsets = grid_points - centre[:, None]
    dipoles = dipole_guess
    charges = base_charge
    for iteration in range(ITERS):
        shared = spread(jnp.concatenate([dipoles, charges.reshape(3, grid_count // 3)], axis=1))
        dipole_tiles = shared[:, :, :, :atom_count].reshape(3, 3 * cell_blocks, BLOCK)
        charge_tiles = jnp.transpose(shared[:, :, :, atom_count:], (1, 2, 0, 3)).reshape(
            3 * cell_gblocks, BLOCK
        )
        local_sums = jnp.concatenate(
            [
                jnp.sum(dipoles, axis=1),
                jnp.sum(charges)[None],
                jnp.sum(charges[None, :] * offsets, axis=1),
            ]
        )
        cell_sums = lax.psum(local_sums, "grp")
        moment_table = lax.all_gather(cell_sums[None, :], "cell", axis=0, tiled=True)
        dipole_sums = moment_table[:, 0:3]
        charge_sums = moment_table[:, 3]
        moments = dipole_sums + moment_table[:, 4:7]
        near_dipoles = listed_tiles(dipole_tiles, atom_lists)
        source_dipoles = listed_tiles(dipole_tiles, source_blocks)
        grid_charges = jnp.take(charge_tiles, grid_blocks, axis=0).reshape(local_blocks, -1)

        def one_atom_block(block_args):
            targets, sources, source_moments, points, point_charges = block_args
            accumulated = dipole_field(targets, sources, source_moments, keep_mask)
            accumulated = accumulated + charge_field(targets, points, point_charges)
            return accumulated + far_field(targets, cell_here, moments, charge_sums)

        def one_grid_block(block_args):
            targets, sources, source_moments = block_args
            return dipole_potential(targets, sources, source_moments) + far_potential(
                targets, cell_here, dipole_sums
            )

        induced_field = lax.map(
            one_atom_block, (atom_targets, near_sites, near_dipoles, grid_sites, grid_charges)
        )
        induced_field = jnp.transpose(induced_field, (1, 0, 2)).reshape(3, atom_count)
        potential = lax.map(one_grid_block, (grid_targets, source_sites, source_dipoles)).reshape(
            grid_count
        )
        dipoles = polarisability[None, :] * (fixed_field + induced_field)
        charges = base_charge - response * potential
    return (dipoles, charges)


def solution(mesh):
    return jax.shard_map(
        body,
        mesh=mesh,
        in_specs=(
            P(None, ("cell", "grp")),
            P(None, ("cell", "grp")),
            P(None, ("cell", "grp")),
            P(None, ("cell", "grp")),
            P(("cell", "grp")),
            P(("cell", "grp")),
            P(("cell", "grp")),
            P(("cell", "grp"), None),
            P(("cell", "grp"), None),
            P(("cell", "grp"), None),
        ),
        out_specs=(P(None, ("cell", "grp")), P(("cell", "grp"))),
        check_vma=False,
    )
```

profile of v0, /device:TPU:0, one launch (start us, length us, event | category | flops | bytes accessed | tf_op | source)
XLA Modules:
  0.0 166.5 jit_solution(10735519480641597523)
XLA Ops:
  1.4 1.3 collective-permute-start.1
  2.7 5.5 %collective-permute-start = (f32[3,1,1,640]{3,0,2,1:T(4,128)S(1)}, f32[3,1,1,640]{3,0,2,1:T(4,128)S(1)}, u32[]{:S(2)}, u32[]{:S(2)}) collective-permute-start(f32[3,1,1,640]{3,0,2,1:T(4,128)S(1)} %maximum_bitcast_fusion.1), channel_id=1, source_target_pairs={{0,4},{4,8},{8,12},{12,16},{16,20},{20,24},{24,28},{1,5},{5,9},{9,... | collective-permute-start | bytes 23048 | tf_op jit(solution)/shard_map/ppermute | solution.py:18
  8.2 1.3 collective-permute-start.3
  9.5 5.4 %collective-permute-start.2 = (f32[3,1,1,896]{3,0,2,1:T(4,128)S(1)}, f32[3,1,1,896]{3,0,2,1:T(4,128)S(1)}, u32[]{:S(2)}, u32[]{:S(2)}) collective-permute-start(f32[3,1,1,896]{3,0,2,1:T(4,128)S(1)} %maximum_bitcast_fusion), channel_id=1, source_target_pairs={{0,4},{4,8},{8,12},{12,16},{16,20},{20,24},{24,28},{1,5},{5,9},{9,... | collective-permute-start | bytes 32264 | tf_op jit(solution)/shard_map/ppermute | solution.py:18
  18.0 5.7 %psum.21 = f32[1,7]{1,0:T(1,128)S(1)} all-reduce(f32[1,7]{1,0:T(1,128)S(1)} %maximum_bitcast_fusion.4), channel_id=1, replica_groups=mesh['cell'=8,'grp'=4] {'grp'}, use_global_device_ids=true, to_apply=%region_3.6 | all-reduce | flops 7 | bytes 56 | tf_op jit(solution)/shard_map/psum | solution.py:183
  24.8 19.3 %all-gather = f32[8,1,7]{2,1,0:T(1,128)S(1)} all-gather(f32[1,1,7]{2,1,0:T(1,128)S(1)} %bitcast.636), channel_id=1, replica_groups=mesh['cell'=8,'grp'=4] {'cell'}, dimensions={0}, use_global_device_ids=true | all-gather | bytes 252 | tf_op jit(solution)/shard_map/all_gather | solution.py:184
  44.6 5.4 %all_gather.21 = f32[3,3,4,640]{3,0,2,1:T(4,128)S(1)} all-gather(f32[3,3,1,640]{3,0,2,1:T(4,128)S(1)} %pad_maximum_fusion.1), channel_id=1, replica_groups=mesh['cell'=8,'grp'=4] {'grp'}, dimensions={2}, use_global_device_ids=true | all-gather | bytes 115200 | tf_op jit(solution)/shard_map/all_gather | solution.py:119
  51.9 5.6 %all_gather.22 = f32[3,3,4,896]{3,0,2,1:T(4,128)S(1)} all-gather(f32[3,3,1,896]{3,0,2,1:T(4,128)S(1)} %pad_maximum_fusion), channel_id=1, replica_groups=mesh['cell'=8,'grp'=4] {'grp'}, dimensions={2}, use_global_device_ids=true | all-gather | bytes 161280 | tf_op jit(solution)/shard_map/all_gather | solution.py:119
  59.7 2.4 %while.79 = (s32[]{:T(128)}, f32[3,128]{1,0:T(4,128)S(1)}, f32[3,3,1024]{2,0,1:T(4,128)S(1)}, f32[3,3,128]{2,1,0:T(4,128)S(1)}, f32[3,3,1024]{2,1,0:T(4,128)S(1)...) while((s32[]{:T(128)}, f32[3,128]{1,0:T(4,128)S(1)}, ...), condition=%wide.region_18.22_spmd, body=%wide.region_15.21_spmd.sunk | while | flops 2375092 | bytes 91217 | solution.py:208
  63.1 6.3 %while.78 = (s32[]{:T(128)}, f32[4,3,128]{2,1,0:T(4,128)S(1)}, f32[4,3,1152]{2,1,0:T(4,128)S(1)}, f32[4,3,128]{2,1,0:T(4,128)S(1)}, f32[4,3,1152]{2,1,0:T(4,128)...) while((s32[]{:T(128)}, f32[4,3,128]{2,1,0:T(4,128)S(1)}, ...), condition=%wide.region_14.17_spmd, body=%wide.region_4.16_spmd.sunk | while | flops 6232500 | bytes 724117 | solution.py:204
  63.7 0.9 fusion.208
  65.3 0.9 fusion.208
  66.9 0.9 fusion.208
  68.5 0.9 fusion.208
  69.6 1.3 collective-permute-start.5
  71.5 4.5 %collective-permute-start.4 = (f32[3,1,1,640]{3,0,2,1:T(4,128)S(1)}, f32[3,1,1,640]{3,0,2,1:T(4,128)S(1)}, u32[]{:S(2)}, u32[]{:S(2)}) collective-permute-start(f32[3,1,1,640]{3,0,2,1:T(4,128)S(1)} %maximum_bitcast_fusion.2), channel_id=1, source_target_pairs={{0,4},{4,8},{8,12},{12,16},{16,20},{20,24},{24,28},{1,5},{5,9},{9,... | collective-permute-start | bytes 23048 | tf_op jit(solution)/shard_map/ppermute | solution.py:18
  76.1 7.0 %psum.22 = f32[1,7]{1,0:T(1,128)S(1)} all-reduce(f32[1,7]{1,0:T(1,128)S(1)} %maximum_bitcast_fusion.5), channel_id=1, replica_groups=mesh['cell'=8,'grp'=4] {'grp'}, use_global_device_ids=true, to_apply=%region_22.26 | all-reduce | flops 7 | bytes 56 | tf_op jit(solution)/shard_map/psum | solution.py:183
  83.1 16.3 %all-gather.1 = f32[8,1,7]{2,1,0:T(1,128)S(1)} all-gather(f32[1,1,7]{2,1,0:T(1,128)S(1)} %bitcast.637), channel_id=1, replica_groups=mesh['cell'=8,'grp'=4] {'cell'}, dimensions={0}, use_global_device_ids=true | all-gather | bytes 252 | tf_op jit(solution)/shard_map/all_gather | solution.py:184
  99.8 5.4 %all_gather.24 = f32[3,3,4,640]{3,0,2,1:T(4,128)S(1)} all-gather(f32[3,3,1,640]{3,0,2,1:T(4,128)S(1)} %pad_maximum_fusion.2), channel_id=1, replica_groups=mesh['cell'=8,'grp'=4] {'grp'}, dimensions={2}, use_global_device_ids=true | all-gather | bytes 115200 | tf_op jit(solution)/shard_map/all_gather | solution.py:119
  107.3 6.3 %while.80 = (s32[]{:T(128)}, f32[4,3,128]{2,1,0:T(4,128)S(1)}, f32[4,3,1152]{2,1,0:T(4,128)S(1)}, f32[4,3,128]{2,1,0:T(4,128)S(1)}, f32[4,3,1152]{2,1,0:T(4,128)...) while((s32[]{:T(128)}, f32[4,3,128]{2,1,0:T(4,128)S(1)}, ...), condition=%wide.region_33.37_spmd, body=%wide.region_23.36_spmd.sunk | while | flops 6232500 | bytes 724117 | solution.py:204
  108.0 0.9 fusion.213
  109.6 0.9 fusion.213
  111.2 0.9 fusion.213
  112.8 0.9 fusion.213
  113.8 2.4 %while.81 = (s32[]{:T(128)}, f32[3,128]{1,0:T(4,128)S(1)}, f32[3,3,1024]{2,0,1:T(4,128)S(1)}, f32[3,3,128]{2,1,0:T(4,128)S(1)}, f32[3,3,1024]{2,1,0:T(4,128)S(1)...) while((s32[]{:T(128)}, f32[3,128]{1,0:T(4,128)S(1)}, ...), condition=%wide.region_37.41_spmd, body=%wide.region_34.40_spmd.sunk | while | flops 2375092 | bytes 91217 | solution.py:208
  117.1 1.3 collective-permute-start.7
  119.1 4.5 %collective-permute-start.6 = (f32[3,1,1,640]{3,0,2,1:T(4,128)S(1)}, f32[3,1,1,640]{3,0,2,1:T(4,128)S(1)}, u32[]{:S(2)}, u32[]{:S(2)}) collective-permute-start(f32[3,1,1,640]{3,0,2,1:T(4,128)S(1)} %maximum_bitcast_fusion.3), channel_id=1, source_target_pairs={{0,4},{4,8},{8,12},{12,16},{16,20},{20,24},{24,28},{1,5},{5,9},{9,... | collective-permute-start | bytes 23048 | tf_op jit(solution)/shard_map/ppermute | solution.py:18
  123.6 5.8 %psum.23 = f32[1,7]{1,0:T(1,128)S(1)} all-reduce(f32[1,7]{1,0:T(1,128)S(1)} %maximum_bitcast_fusion.6), channel_id=1, replica_groups=mesh['cell'=8,'grp'=4] {'grp'}, use_global_device_ids=true, to_apply=%region_41.45 | all-reduce | flops 7 | bytes 56 | tf_op jit(solution)/shard_map/psum | solution.py:183
  129.4 19.2 %all-gather.2 = f32[8,1,7]{2,1,0:T(1,128)S(1)} all-gather(f32[1,1,7]{2,1,0:T(1,128)S(1)} %bitcast.638), channel_id=1, replica_groups=mesh['cell'=8,'grp'=4] {'cell'}, dimensions={0}, use_global_device_ids=true | all-gather | bytes 252 | tf_op jit(solution)/shard_map/all_gather | solution.py:184
  149.0 5.4 %all_gather.26 = f32[3,3,4,640]{3,0,2,1:T(4,128)S(1)} all-gather(f32[3,3,1,640]{3,0,2,1:T(4,128)S(1)} %pad_maximum_fusion.3), channel_id=1, replica_groups=mesh['cell'=8,'grp'=4] {'grp'}, dimensions={2}, use_global_device_ids=true | all-gather | bytes 115200 | tf_op jit(solution)/shard_map/all_gather | solution.py:119
  156.5 6.3 %while.82 = (s32[]{:T(128)}, f32[4,3,128]{2,1,0:T(4,128)S(1)}, f32[4,3,1152]{2,1,0:T(4,128)S(1)}, f32[4,3,128]{2,1,0:T(4,128)S(1)}, f32[4,3,1152]{2,1,0:T(4,128)...) while((s32[]{:T(128)}, f32[4,3,128]{2,1,0:T(4,128)S(1)}, ...), condition=%wide.region_52.56_spmd, body=%wide.region_42.55_spmd.sunk | while | flops 6232500 | bytes 724117 | solution.py:204
  163.5 2.4 %while.83 = (s32[]{:T(128)}, f32[3,128]{1,0:T(4,128)S(1)}, f32[3,3,1024]{2,0,1:T(4,128)S(1)}, f32[3,3,128]{2,1,0:T(4,128)S(1)}, f32[3,3,1024]{2,1,0:T(4,128)S(1)...) while((s32[]{:T(128)}, f32[3,128]{1,0:T(4,128)S(1)}, ...), condition=%wide.region_56.60_spmd, body=%wide.region_53.59_spmd.sunk | while | flops 2375092 | bytes 91217 | solution.py:208
  (386 shorter events, 36.3 us)
Async XLA Ops:
  0.6 7.5 %copy-start = (f32[3,384]{1,0:T(4,128)S(1)}, f32[3,384]{1,0:T(4,128)}, u32[]{:S(2)}) copy-start(f32[3,384]{1,0:T(4,128)} %param.29) | copy-start | bytes 13828
  0.6 7.5 %copy-start.1 = (f32[3,512]{1,0:T(4,128)S(1)}, f32[3,512]{1,0:T(4,128)}, u32[]{:S(2)}) copy-start(f32[3,512]{1,0:T(4,128)} %param.28) | copy-start | bytes 18436
  1.4 43.2 %collective-permute-start.1 = (f32[3,1,1,640]{3,0,2,1:T(4,128)S(1)}, f32[3,1,1,640]{3,0,2,1:T(4,128)S(1)}, u32[]{:S(2)}, u32[]{:S(2)}) collective-permute-start(f32[3,1,1,640]{3,0,2,1:T(4,128)S(1)} %maximum_bitcast_fusion.1), channel_id=1, source_target_pairs={{4,0},{8,4},{12,8},{16,12},{20,16},{24,20},{28,24},{5,1},{9,5},{13... | collective-permute-start | bytes 23048 | tf_op jit(solution)/shard_map/ppermute | solution.py:19
  2.7 41.9 %collective-permute-start = (f32[3,1,1,640]{3,0,2,1:T(4,128)S(1)}, f32[3,1,1,640]{3,0,2,1:T(4,128)S(1)}, u32[]{:S(2)}, u32[]{:S(2)}) collective-permute-start(f32[3,1,1,640]{3,0,2,1:T(4,128)S(1)} %maximum_bitcast_fusion.1), channel_id=1, source_target_pairs={{0,4},{4,8},{8,12},{12,16},{16,20},{20,24},{24,28},{1,5},{5,9},{9,... | collective-permute-start | bytes 23048 | tf_op jit(solution)/shard_map/ppermute | solution.py:18
  8.2 6.8 %copy-start.7 = (s32[4,4]{1,0:T(4,128)S(1)}, s32[4,4]{1,0:T(4,128)}, u32[]{:S(2)}) copy-start(s32[4,4]{1,0:T(4,128)} %param.36) | copy-start | bytes 196
  8.2 43.7 %collective-permute-start.3 = (f32[3,1,1,896]{3,0,2,1:T(4,128)S(1)}, f32[3,1,1,896]{3,0,2,1:T(4,128)S(1)}, u32[]{:S(2)}, u32[]{:S(2)}) collective-permute-start(f32[3,1,1,896]{3,0,2,1:T(4,128)S(1)} %maximum_bitcast_fusion), channel_id=1, source_target_pairs={{4,0},{8,4},{12,8},{16,12},{20,16},{24,20},{28,24},{5,1},{9,5},{13... | collective-permute-start | bytes 32264 | tf_op jit(solution)/shard_map/ppermute | solution.py:19
  9.5 42.4 %collective-permute-start.2 = (f32[3,1,1,896]{3,0,2,1:T(4,128)S(1)}, f32[3,1,1,896]{3,0,2,1:T(4,128)S(1)}, u32[]{:S(2)}, u32[]{:S(2)}) collective-permute-start(f32[3,1,1,896]{3,0,2,1:T(4,128)S(1)} %maximum_bitcast_fusion), channel_id=1, source_target_pairs={{0,4},{4,8},{8,12},{12,16},{16,20},{20,24},{24,28},{1,5},{5,9},{9,... | collective-permute-start | bytes 32264 | tf_op jit(solution)/shard_map/ppermute | solution.py:18
  15.0 0.7 copy-start.8
  15.7 0.7 copy-start.2
  15.7 1.3 copy-start.4
  23.8 0.7 copy-start.9
  59.6 2.4 %copy-start.5 = (f32[384]{0:T(512)S(1)}, f32[384]{0:T(512)}, u32[]{:S(2)}) copy-start(f32[384]{0:T(512)} %param.34) | copy-start | bytes 4612
  63.0 6.4 %copy-start.3 = (f32[3,512]{1,0:T(4,128)S(1)}, f32[3,512]{1,0:T(4,128)}, u32[]{:S(2)}) copy-start(f32[3,512]{1,0:T(4,128)} %param.31) | copy-start | bytes 18436
  63.0 6.4 %copy-start.6 = (f32[512]{0:T(512)S(1)}, f32[512]{0:T(512)}, u32[]{:S(2)}) copy-start(f32[512]{0:T(512)} %param.32) | copy-start | bytes 6148
  69.6 30.3 %collective-permute-start.5 = (f32[3,1,1,640]{3,0,2,1:T(4,128)S(1)}, f32[3,1,1,640]{3,0,2,1:T(4,128)S(1)}, u32[]{:S(2)}, u32[]{:S(2)}) collective-permute-start(f32[3,1,1,640]{3,0,2,1:T(4,128)S(1)} %maximum_bitcast_fusion.2), channel_id=1, source_target_pairs={{4,0},{8,4},{12,8},{16,12},{20,16},{24,20},{28,24},{5,1},{9,5},{13... | collective-permute-start | bytes 23048 | tf_op jit(solution)/shard_map/ppermute | solution.py:19
  71.5 28.3 %collective-permute-start.4 = (f32[3,1,1,640]{3,0,2,1:T(4,128)S(1)}, f32[3,1,1,640]{3,0,2,1:T(4,128)S(1)}, u32[]{:S(2)}, u32[]{:S(2)}) collective-permute-start(f32[3,1,1,640]{3,0,2,1:T(4,128)S(1)} %maximum_bitcast_fusion.2), channel_id=1, source_target_pairs={{0,4},{4,8},{8,12},{12,16},{16,20},{20,24},{24,28},{1,5},{5,9},{9,... | collective-permute-start | bytes 23048 | tf_op jit(solution)/shard_map/ppermute | solution.py:18
  117.1 31.9 %collective-permute-start.7 = (f32[3,1,1,640]{3,0,2,1:T(4,128)S(1)}, f32[3,1,1,640]{3,0,2,1:T(4,128)S(1)}, u32[]{:S(2)}, u32[]{:S(2)}) collective-permute-start(f32[3,1,1,640]{3,0,2,1:T(4,128)S(1)} %maximum_bitcast_fusion.3), channel_id=1, source_target_pairs={{4,0},{8,4},{12,8},{16,12},{20,16},{24,20},{28,24},{5,1},{9,5},{13... | collective-permute-start | bytes 23048 | tf_op jit(solution)/shard_map/ppermute | solution.py:19
  119.1 29.9 %collective-permute-start.6 = (f32[3,1,1,640]{3,0,2,1:T(4,128)S(1)}, f32[3,1,1,640]{3,0,2,1:T(4,128)S(1)}, u32[]{:S(2)}, u32[]{:S(2)}) collective-permute-start(f32[3,1,1,640]{3,0,2,1:T(4,128)S(1)} %maximum_bitcast_fusion.3), channel_id=1, source_target_pairs={{0,4},{4,8},{8,12},{12,16},{16,20},{20,24},{24,28},{1,5},{5,9},{9,... | collective-permute-start | bytes 23048 | tf_op jit(solution)/shard_map/ppermute | solution.py:18
where the time goes:
time: 167 us; the launch traced here: 166 us
  blocking collectives  95.1 us (57%)
  other arithmetic  30.4 us (18%)
  starting transfers between devices  25.2 us (15%)
  local copies, waits for them, and re-layouts  13.1 us (8%)
    all_gather x3, blocking collectives, body(): lax.all_gather(cell_sums[None, :], 'cell', axis=0, tiled=True)  54.8 us
    all_gather x4, blocking collectives, spread(): return lax.all_gather(with_rims, 'grp', axis=2, tiled=True)  21.7 us
    ppermute x4, starting transfers between devices, with_halo(): before = lax.ppermute(last, axis, up)  20 us
    psum x3, blocking collectives, body(): cell_sums = lax.psum(local_sums, 'grp')  18.6 us
    reduce_sum x12, other arithmetic, dipole_field(): jnp.sum(radial * delta_x - moments[0][None, :] * direct, axis=1)  10.7 us
    gather x10, local copies, waits for them, and re-layouts, listed_tiles(): taken = jnp.take(tile_set, index_lists, axis=1)  5.42 us
    ppermute x4, starting transfers between devices, with_halo(): after = lax.ppermute(initial, axis, down)  5.16 us
    reduce_sum x9, other arithmetic, dipole_potential(): return jnp.sum(projected * inv_cube, axis=1)  4.71 us
  transfers between devices with their start and end apart: 8, of which 0 were waited for; matrix products, arithmetic and copies ran while one was open for 4% of the time, Pallas kernels for 0%

commit v1 on v0

--- a/solution.py
+++ b/solution.py
@@ -180,7 +180,8 @@
                 jnp.sum(charges[None, :] * offsets, axis=1),
             ]
         )
-        cell_sums = lax.psum(local_sums, "grp")
+        parts = lax.all_gather(local_sums, "grp", axis=0, tiled=False)
+        cell_sums = parts.sum(axis=0)
         moment_table = lax.all_gather(cell_sums[None, :], "cell", axis=0, tiled=True)
         dipole_sums = moment_table[:, 0:3]
         charge_sums = moment_table[:, 3]

time: 167 us -> 174 us (1.042)
  local copies, waits for them, and re-layouts: 13.1 us -> 16.1 us
  blocking collectives: 95.1 us -> 97.5 us
    unnamed x0 -> x6, blocking collectives: none -> 75.8 us
    all_gather x3 -> x0, blocking collectives: 54.8 us -> none  [body(): lax.all_gather(cell_sums[None, :], 'cell', axis=0, tiled=True)]
    psum x3 -> x0, blocking collectives: 18.6 us -> none  [body(): cell_sums = lax.psum(local_sums, 'grp')]
    unnamed x23 -> x38, local copies, waits for them, and re-layouts: 2.06 us -> 4.57 us
    unnamed x3 -> x6, other arithmetic: 0.23 us -> 2.64 us
    broadcast_in_dim x3 -> x0, other arithmetic: 2.13 us -> none  [body(): cell_sums[None, :]]
  transfers between devices with their start and end apart: 8 -> 8, of which waited for: 0 -> 0; matrix products, arithmetic and copies ran while one was open for 4% -> 5% of each run, Pallas kernels for 0% -> 0%
where the time goes in v1:
time: 174 us
  blocking collectives  97.5 us (56%)
  other arithmetic  30.7 us (18%)
  starting transfers between devices  25.2 us (14%)
  local copies, waits for them, and re-layouts  16.1 us (9%)
  between operations  2.54 us (1%)
    unnamed x6, blocking collectives  75.8 us
    all_gather x4, blocking collectives, spread(): return lax.all_gather(with_rims, 'grp', axis=2, tiled=True)  21.7 us
    ppermute x4, starting transfers between devices, with_halo(): before = lax.ppermute(last, axis, up)  20 us
    reduce_sum x12, other arithmetic, dipole_field(): jnp.sum(radial * delta_x - moments[0][None, :] * direct, axis=1)  10.7 us
    gather x10, local copies, waits for them, and re-layouts, listed_tiles(): taken = jnp.take(tile_set, index_lists, axis=1)  5.42 us
    ppermute x4, starting transfers between devices, with_halo(): after = lax.ppermute(initial, axis, down)  5.16 us
    reduce_sum x9, other arithmetic, dipole_potential(): return jnp.sum(projected * inv_cube, axis=1)  4.71 us
    unnamed x38, local copies, waits for them, and re-layouts  4.57 us
  transfers between devices with their start and end apart: 8, of which 0 were waited for; matrix products, arithmetic and copies ran while one was open for 5% of the time, Pallas kernels for 0%

profile of v1, /device:TPU:0, one launch (start us, length us, event | category | flops | bytes accessed | tf_op | source)
XLA Modules:
  0.0 173.7 jit_solution(18302989412209890871)
XLA Ops:
  1.4 1.3 collective-permute-start.1
  2.7 5.5 %collective-permute-start = (f32[3,1,1,640]{3,0,2,1:T(4,128)S(1)}, f32[3,1,1,640]{3,0,2,1:T(4,128)S(1)}, u32[]{:S(2)}, u32[]{:S(2)}) collective-permute-start(f32[3,1,1,640]{3,0,2,1:T(4,128)S(1)} %maximum_bitcast_fusion.1), channel_id=1, source_target_pairs={{0,4},{4,8},{8,12},{12,16},{16,20},{20,24},{24,28},{1,5},{5,9},{9,... | collective-permute-start | bytes 23048 | tf_op jit(solution)/shard_map/ppermute | solution.py:18
  8.2 1.3 collective-permute-start.3
  9.5 5.4 %collective-permute-start.2 = (f32[3,1,1,896]{3,0,2,1:T(4,128)S(1)}, f32[3,1,1,896]{3,0,2,1:T(4,128)S(1)}, u32[]{:S(2)}, u32[]{:S(2)}) collective-permute-start(f32[3,1,1,896]{3,0,2,1:T(4,128)S(1)} %maximum_bitcast_fusion), channel_id=1, source_target_pairs={{0,4},{4,8},{8,12},{12,16},{16,20},{20,24},{24,28},{1,5},{5,9},{9,... | collective-permute-start | bytes 32264 | tf_op jit(solution)/shard_map/ppermute | solution.py:18
  21.3 5.7 %all-reduce.2 = f32[28]{0:T(128)S(1)} all-reduce(f32[28]{0:T(128)S(1)} %maximum_dynamic-update-slice_fusion), channel_id=2, replica_groups=mesh['cell'=8,'grp'=4] {'grp'}, use_global_device_ids=true, to_apply=%add.2 | all-reduce | flops 28 | bytes 224
  27.4 20.1 %all-reduce.3 = f32[56]{0:T(128)S(1)} all-reduce(f32[56]{0:T(128)S(1)} %dynamic-update-slice.1), channel_id=3, replica_groups=mesh['cell'=8,'grp'=4] {'cell'}, use_global_device_ids=true, to_apply=%add.3 | all-reduce | flops 56 | bytes 448
  49.1 5.4 %all_gather.39 = f32[3,3,4,640]{3,0,2,1:T(4,128)S(1)} all-gather(f32[3,3,1,640]{3,0,2,1:T(4,128)S(1)} %pad_maximum_fusion.1), channel_id=1, replica_groups=mesh['cell'=8,'grp'=4] {'grp'}, dimensions={2}, use_global_device_ids=true | all-gather | bytes 115200 | tf_op jit(solution)/shard_map/all_gather | solution.py:119
  56.5 5.6 %all_gather.40 = f32[3,3,4,896]{3,0,2,1:T(4,128)S(1)} all-gather(f32[3,3,1,896]{3,0,2,1:T(4,128)S(1)} %pad_maximum_fusion), channel_id=1, replica_groups=mesh['cell'=8,'grp'=4] {'grp'}, dimensions={2}, use_global_device_ids=true | all-gather | bytes 161280 | tf_op jit(solution)/shard_map/all_gather | solution.py:119
  64.2 2.4 %while.79 = (s32[]{:T(128)}, f32[3,128]{1,0:T(4,128)S(1)}, f32[3,3,1024]{2,0,1:T(4,128)S(1)}, f32[3,3,128]{2,1,0:T(4,128)S(1)}, f32[3,3,1024]{2,1,0:T(4,128)S(1)...) while((s32[]{:T(128)}, f32[3,128]{1,0:T(4,128)S(1)}, ...), condition=%wide.region_18.22_spmd, body=%wide.region_15.21_spmd.sunk | while | flops 2375092 | bytes 91217 | solution.py:209
  67.6 6.3 %while.78 = (s32[]{:T(128)}, f32[4,3,128]{2,1,0:T(4,128)S(1)}, f32[4,3,1152]{2,1,0:T(4,128)S(1)}, f32[4,3,128]{2,1,0:T(4,128)S(1)}, f32[4,3,1152]{2,1,0:T(4,128)...) while((s32[]{:T(128)}, f32[4,3,128]{2,1,0:T(4,128)S(1)}, ...), condition=%wide.region_14.17_spmd, body=%wide.region_4.16_spmd.sunk | while | flops 6232500 | bytes 724117 | solution.py:205
  68.2 0.9 fusion.208
  69.8 0.9 fusion.208
  71.4 0.9 fusion.208
  73.0 0.9 fusion.208
  74.1 1.3 collective-permute-start.5
  75.4 4.5 %collective-permute-start.4 = (f32[3,1,1,640]{3,0,2,1:T(4,128)S(1)}, f32[3,1,1,640]{3,0,2,1:T(4,128)S(1)}, u32[]{:S(2)}, u32[]{:S(2)}) collective-permute-start(f32[3,1,1,640]{3,0,2,1:T(4,128)S(1)} %maximum_bitcast_fusion.2), channel_id=1, source_target_pairs={{0,4},{4,8},{8,12},{12,16},{16,20},{20,24},{24,28},{1,5},{5,9},{9,... | collective-permute-start | bytes 23048 | tf_op jit(solution)/shard_map/ppermute | solution.py:18
  80.7 7.0 %all-reduce.4 = f32[28]{0:T(128)S(1)} all-reduce(f32[28]{0:T(128)S(1)} %maximum_dynamic-update-slice_fusion.1), channel_id=4, replica_groups=mesh['cell'=8,'grp'=4] {'grp'}, use_global_device_ids=true, to_apply=%add.4 | all-reduce | flops 28 | bytes 224
  88.1 17.1 %all-reduce.5 = f32[56]{0:T(128)S(1)} all-reduce(f32[56]{0:T(128)S(1)} %dynamic-update-slice.3), channel_id=5, replica_groups=mesh['cell'=8,'grp'=4] {'cell'}, use_global_device_ids=true, to_apply=%add.5 | all-reduce | flops 56 | bytes 448
  105.7 5.4 %all_gather.44 = f32[3,3,4,640]{3,0,2,1:T(4,128)S(1)} all-gather(f32[3,3,1,640]{3,0,2,1:T(4,128)S(1)} %pad_maximum_fusion.2), channel_id=1, replica_groups=mesh['cell'=8,'grp'=4] {'grp'}, dimensions={2}, use_global_device_ids=true | all-gather | bytes 115200 | tf_op jit(solution)/shard_map/all_gather | solution.py:119
  113.2 6.3 %while.80 = (s32[]{:T(128)}, f32[4,3,128]{2,1,0:T(4,128)S(1)}, f32[4,3,1152]{2,1,0:T(4,128)S(1)}, f32[4,3,128]{2,1,0:T(4,128)S(1)}, f32[4,3,1152]{2,1,0:T(4,128)...) while((s32[]{:T(128)}, f32[4,3,128]{2,1,0:T(4,128)S(1)}, ...), condition=%wide.region_33.37_spmd, body=%wide.region_23.36_spmd.sunk | while | flops 6232500 | bytes 724117 | solution.py:205
  113.9 0.9 fusion.213
  115.5 0.9 fusion.213
  117.1 0.9 fusion.213
  118.6 0.9 fusion.213
  119.7 2.4 %while.81 = (s32[]{:T(128)}, f32[3,128]{1,0:T(4,128)S(1)}, f32[3,3,1024]{2,0,1:T(4,128)S(1)}, f32[3,3,128]{2,1,0:T(4,128)S(1)}, f32[3,3,1024]{2,1,0:T(4,128)S(1)...) while((s32[]{:T(128)}, f32[3,128]{1,0:T(4,128)S(1)}, ...), condition=%wide.region_37.41_spmd, body=%wide.region_34.40_spmd.sunk | while | flops 2375092 | bytes 91217 | solution.py:209
  122.9 1.3 collective-permute-start.7
  124.2 4.5 %collective-permute-start.6 = (f32[3,1,1,640]{3,0,2,1:T(4,128)S(1)}, f32[3,1,1,640]{3,0,2,1:T(4,128)S(1)}, u32[]{:S(2)}, u32[]{:S(2)}) collective-permute-start(f32[3,1,1,640]{3,0,2,1:T(4,128)S(1)} %maximum_bitcast_fusion.3), channel_id=1, source_target_pairs={{0,4},{4,8},{8,12},{12,16},{16,20},{20,24},{24,28},{1,5},{5,9},{9,... | collective-permute-start | bytes 23048 | tf_op jit(solution)/shard_map/ppermute | solution.py:18
  129.6 5.7 %all-reduce.6 = f32[28]{0:T(128)S(1)} all-reduce(f32[28]{0:T(128)S(1)} %maximum_dynamic-update-slice_fusion.2), channel_id=6, replica_groups=mesh['cell'=8,'grp'=4] {'grp'}, use_global_device_ids=true, to_apply=%add.6 | all-reduce | flops 28 | bytes 224
  135.7 20.0 %all-reduce.7 = f32[56]{0:T(128)S(1)} all-reduce(f32[56]{0:T(128)S(1)} %dynamic-update-slice.5), channel_id=7, replica_groups=mesh['cell'=8,'grp'=4] {'cell'}, use_global_device_ids=true, to_apply=%add.7 | all-reduce | flops 56 | bytes 448
  156.2 5.4 %all_gather.48 = f32[3,3,4,640]{3,0,2,1:T(4,128)S(1)} all-gather(f32[3,3,1,640]{3,0,2,1:T(4,128)S(1)} %pad_maximum_fusion.3), channel_id=1, replica_groups=mesh['cell'=8,'grp'=4] {'grp'}, dimensions={2}, use_global_device_ids=true | all-gather | bytes 115200 | tf_op jit(solution)/shard_map/all_gather | solution.py:119
  163.7 6.3 %while.82 = (s32[]{:T(128)}, f32[4,3,128]{2,1,0:T(4,128)S(1)}, f32[4,3,1152]{2,1,0:T(4,128)S(1)}, f32[4,3,128]{2,1,0:T(4,128)S(1)}, f32[4,3,1152]{2,1,0:T(4,128)...) while((s32[]{:T(128)}, f32[4,3,128]{2,1,0:T(4,128)S(1)}, ...), condition=%wide.region_52.56_spmd, body=%wide.region_42.55_spmd.sunk | while | flops 6232500 | bytes 724117 | solution.py:205
  170.7 2.4 %while.83 = (s32[]{:T(128)}, f32[3,128]{1,0:T(4,128)S(1)}, f32[3,3,1024]{2,0,1:T(4,128)S(1)}, f32[3,3,128]{2,1,0:T(4,128)S(1)}, f32[3,3,1024]{2,1,0:T(4,128)S(1)...) while((s32[]{:T(128)}, f32[3,128]{1,0:T(4,128)S(1)}, ...), condition=%wide.region_56.60_spmd, body=%wide.region_53.59_spmd.sunk | while | flops 2375092 | bytes 91217 | solution.py:209
  (410 shorter events, 39.7 us)
Async XLA Ops:
  0.6 7.5 %copy-start = (f32[3,384]{1,0:T(4,128)S(1)}, f32[3,384]{1,0:T(4,128)}, u32[]{:S(2)}) copy-start(f32[3,384]{1,0:T(4,128)} %param.29) | copy-start | bytes 13828
  0.6 7.5 %copy-start.1 = (f32[3,512]{1,0:T(4,128)S(1)}, f32[3,512]{1,0:T(4,128)}, u32[]{:S(2)}) copy-start(f32[3,512]{1,0:T(4,128)} %param.28) | copy-start | bytes 18436
  1.4 47.7 %collective-permute-start.1 = (f32[3,1,1,640]{3,0,2,1:T(4,128)S(1)}, f32[3,1,1,640]{3,0,2,1:T(4,128)S(1)}, u32[]{:S(2)}, u32[]{:S(2)}) collective-permute-start(f32[3,1,1,640]{3,0,2,1:T(4,128)S(1)} %maximum_bitcast_fusion.1), channel_id=1, source_target_pairs={{4,0},{8,4},{12,8},{16,12},{20,16},{24,20},{28,24},{5,1},{9,5},{13... | collective-permute-start | bytes 23048 | tf_op jit(solution)/shard_map/ppermute | solution.py:19
  2.7 46.4 %collective-permute-start = (f32[3,1,1,640]{3,0,2,1:T(4,128)S(1)}, f32[3,1,1,640]{3,0,2,1:T(4,128)S(1)}, u32[]{:S(2)}, u32[]{:S(2)}) collective-permute-start(f32[3,1,1,640]{3,0,2,1:T(4,128)S(1)} %maximum_bitcast_fusion.1), channel_id=1, source_target_pairs={{0,4},{4,8},{8,12},{12,16},{16,20},{20,24},{24,28},{1,5},{5,9},{9,... | collective-permute-start | bytes 23048 | tf_op jit(solution)/shard_map/ppermute | solution.py:18
  8.2 6.8 %copy-start.7 = (s32[4,4]{1,0:T(4,128)S(1)}, s32[4,4]{1,0:T(4,128)}, u32[]{:S(2)}) copy-start(s32[4,4]{1,0:T(4,128)} %param.36) | copy-start | bytes 196
  8.2 48.2 %collective-permute-start.3 = (f32[3,1,1,896]{3,0,2,1:T(4,128)S(1)}, f32[3,1,1,896]{3,0,2,1:T(4,128)S(1)}, u32[]{:S(2)}, u32[]{:S(2)}) collective-permute-start(f32[3,1,1,896]{3,0,2,1:T(4,128)S(1)} %maximum_bitcast_fusion), channel_id=1, source_target_pairs={{4,0},{8,4},{12,8},{16,12},{20,16},{24,20},{28,24},{5,1},{9,5},{13... | collective-permute-start | bytes 32264 | tf_op jit(solution)/shard_map/ppermute | solution.py:19
  9.5 46.9 %collective-permute-start.2 = (f32[3,1,1,896]{3,0,2,1:T(4,128)S(1)}, f32[3,1,1,896]{3,0,2,1:T(4,128)S(1)}, u32[]{:S(2)}, u32[]{:S(2)}) collective-permute-start(f32[3,1,1,896]{3,0,2,1:T(4,128)S(1)} %maximum_bitcast_fusion), channel_id=1, source_target_pairs={{0,4},{4,8},{8,12},{12,16},{16,20},{20,24},{24,28},{1,5},{5,9},{9,... | collective-permute-start | bytes 32264 | tf_op jit(solution)/shard_map/ppermute | solution.py:18
  15.0 0.7 copy-start.8
  15.7 0.7 copy-start.2
  15.8 1.3 copy-start.4
  17.0 0.7 copy-start.11
  17.7 0.7 copy-start.10
  47.5 0.7 copy-start.9
  64.2 2.4 %copy-start.5 = (f32[384]{0:T(512)S(1)}, f32[384]{0:T(512)}, u32[]{:S(2)}) copy-start(f32[384]{0:T(512)} %param.34) | copy-start | bytes 4612
  67.5 6.4 %copy-start.3 = (f32[3,512]{1,0:T(4,128)S(1)}, f32[3,512]{1,0:T(4,128)}, u32[]{:S(2)}) copy-start(f32[3,512]{1,0:T(4,128)} %param.31) | copy-start | bytes 18436
  67.5 6.4 %copy-start.6 = (f32[512]{0:T(512)S(1)}, f32[512]{0:T(512)}, u32[]{:S(2)}) copy-start(f32[512]{0:T(512)} %param.32) | copy-start | bytes 6148
  74.1 31.6 %collective-permute-start.5 = (f32[3,1,1,640]{3,0,2,1:T(4,128)S(1)}, f32[3,1,1,640]{3,0,2,1:T(4,128)S(1)}, u32[]{:S(2)}, u32[]{:S(2)}) collective-permute-start(f32[3,1,1,640]{3,0,2,1:T(4,128)S(1)} %maximum_bitcast_fusion.2), channel_id=1, source_target_pairs={{4,0},{8,4},{12,8},{16,12},{20,16},{24,20},{28,24},{5,1},{9,5},{13... | collective-permute-start | bytes 23048 | tf_op jit(solution)/shard_map/ppermute | solution.py:19
  75.4 30.3 %collective-permute-start.4 = (f32[3,1,1,640]{3,0,2,1:T(4,128)S(1)}, f32[3,1,1,640]{3,0,2,1:T(4,128)S(1)}, u32[]{:S(2)}, u32[]{:S(2)}) collective-permute-start(f32[3,1,1,640]{3,0,2,1:T(4,128)S(1)} %maximum_bitcast_fusion.2), channel_id=1, source_target_pairs={{0,4},{4,8},{8,12},{12,16},{16,20},{20,24},{24,28},{1,5},{5,9},{9,... | collective-permute-start | bytes 23048 | tf_op jit(solution)/shard_map/ppermute | solution.py:18
  122.9 33.3 %collective-permute-start.7 = (f32[3,1,1,640]{3,0,2,1:T(4,128)S(1)}, f32[3,1,1,640]{3,0,2,1:T(4,128)S(1)}, u32[]{:S(2)}, u32[]{:S(2)}) collective-permute-start(f32[3,1,1,640]{3,0,2,1:T(4,128)S(1)} %maximum_bitcast_fusion.3), channel_id=1, source_target_pairs={{4,0},{8,4},{12,8},{16,12},{20,16},{24,20},{28,24},{5,1},{9,5},{13... | collective-permute-start | bytes 23048 | tf_op jit(solution)/shard_map/ppermute | solution.py:19
  124.2 32.0 %collective-permute-start.6 = (f32[3,1,1,640]{3,0,2,1:T(4,128)S(1)}, f32[3,1,1,640]{3,0,2,1:T(4,128)S(1)}, u32[]{:S(2)}, u32[]{:S(2)}) collective-permute-start(f32[3,1,1,640]{3,0,2,1:T(4,128)S(1)} %maximum_bitcast_fusion.3), channel_id=1, source_target_pairs={{0,4},{4,8},{8,12},{12,16},{16,20},{20,24},{24,28},{1,5},{5,9},{9,... | collective-permute-start | bytes 23048 | tf_op jit(solution)/shard_map/ppermute | solution.py:18
